TPU v7x, 32 devices: a whole 2x2x4 slice. The times are simulated.
32 devices in a mesh: fsdp: 4 (over z), seq: 8 (over y, x, core).
Axes of the slice: x: 2, y: 2, z: 4, core: 2. Of those that a mesh axis runs over, the one named last changes fastest.
Arguments:
- timestep: int32 [4], P('fsdp'), may hold values from 0 to 999
- pooled: bfloat16 [4, 3072], P('fsdp'), may hold values from -6 to 6
- modulation_weight: bfloat16 [3072, 9216], P('fsdp', 'seq'), may hold values from -0.109375 to 0.109375
- reference_attention: bfloat16 [4, 2, 512, 1536], P('fsdp', None, 'seq'), may hold values from -6 to 6
- policy_attention: bfloat16 [4, 2, 512, 1536], P('fsdp', None, 'seq'), may hold values from -6 to 6
- reference_residual: bfloat16 [4, 2, 512, 3072], P('fsdp', None, 'seq'), may hold values from -6 to 6
- policy_residual: bfloat16 [4, 2, 512, 3072], P('fsdp', None, 'seq'), may hold values from -6 to 6
- noise: float32 [4, 2, 512, 64], P('fsdp', None, 'seq'), may hold values from -6 to 6
- latent: float32 [4, 2, 512, 64], P('fsdp', None, 'seq'), may hold values from -3 to 3
- frozen_output_weight: bfloat16 [1536, 3072], P(None, 'fsdp'), may hold values from -0.15625 to 0.15625
- adapter_down_weight: bfloat16 [64, 1536], P(None, 'fsdp'), may hold values from -0.15625 to 0.15625
- adapter_up_weight: bfloat16 [64, 3072], P(None, 'fsdp'), may hold values from -0.75 to 0.75
- reference_head: bfloat16 [64, 3072], P(None, 'fsdp'), may hold values from -0.109375 to 0.109375
- policy_head: bfloat16 [64, 3072], P(None, 'fsdp'), may hold values from -0.109375 to 0.109375
Outputs:
- loss: float32 [4], P('fsdp')
- grad_down: float32 [64, 1536], P(None, 'fsdp')
- grad_up: float32 [64, 3072], P(None, 'fsdp')
- grad_head: float32 [64, 3072], P(None, 'fsdp')
- grad_resid: bfloat16 [4, 2, 512, 3072], P('fsdp', None, 'seq')
- grad_attn: bfloat16 [4, 2, 512, 1536], P('fsdp', None, 'seq')
All inputs are finite; a program needn't handle non-finite values.
Results may differ from a plain program's by a relative error of at most 0.029.
Values may be sent and summed in bfloat16 or wider, within the bound.
No kernel may reach another device: no remote copies, remote signals or barrier semaphores. Data moves between devices by JAX's collectives and lax.ppermute only.
A program may use at most 64 MiB of HBM per device.

v0:
```python
import math
import jax
import jax.numpy as jnp
from jax import lax
from jax.sharding import PartitionSpec as P

EPSILON = 1e-06


def embedding(timestep, layer_width):
    half_width = layer_width // 2
    frequency = jnp.exp(-math.log(10000.0) * jnp.arange(half_width, dtype=jnp.float32) / half_width)
    angles = timestep.astype(jnp.float32)[:, None] * frequency[None, :]
    return jnp.concatenate([jnp.cos(angles), jnp.sin(angles)], axis=1)


def contract_rows(left, right):
    return lax.dot_general(
        left, right, (((0,), (0,)), ((), ())), preferred_element_type=jnp.float32
    )


def contracted_columns(left, right):
    return lax.dot_general(
        left, right, (((1,), (1,)), ((), ())), preferred_element_type=jnp.float32
    )


def final_layer(projected, residual, gate_row, shift_row, scale_row, head):
    stream = residual.astype(jnp.float32) + gate_row * projected
    row_mean = jnp.mean(stream, axis=1, keepdims=True)
    centred = stream - row_mean
    variance = jnp.mean(centred * centred, axis=1, keepdims=True)
    inv_std = lax.rsqrt(variance + EPSILON)
    normed = centred * inv_std
    modulated = (normed * (1.0 + scale_row) + shift_row).astype(jnp.bfloat16)
    predicted = contracted_columns(modulated, head)
    return (normed, inv_std, modulated, predicted)


def member_errors(predicted, target, scale_total):
    offset = predicted - target
    squared = jnp.sum(offset * offset, axis=1)
    return jnp.sum(squared.reshape(2, -1), axis=1) / scale_total


def local(
    timestep,
    pooled,
    modulation_weight,
    reference_attention,
    policy_attention,
    reference_residual,
    policy_residual,
    noise,
    latent,
    frozen_output_weight,
    adapter_down_weight,
    adapter_up_weight,
    reference_head,
    policy_head,
):
    layer_width = pooled.shape[1]
    feature_index = reference_attention.shape[-1]
    channel_count = noise.shape[-1]
    tok_seq = reference_attention.shape[2]
    length = tok_seq * lax.axis_size("seq")
    scale_total = float(length * channel_count)
    beta = math.sqrt(length * channel_count) / 8.0
    cond_vec = pooled.astype(jnp.float32) + embedding(timestep, layer_width)
    activated = jax.nn.silu(cond_vec).astype(jnp.bfloat16)
    pieces = lax.all_to_all(activated, "fsdp", split_axis=1, concat_axis=0, tiled=True)
    partial_value = jnp.dot(pieces, modulation_weight, preferred_element_type=jnp.float32)
    own_part = lax.psum_scatter(partial_value, "fsdp", scatter_dimension=0, tiled=True)
    modulation = lax.all_gather(own_part, "seq", axis=1, tiled=True)
    gate_row = modulation[:, :layer_width]
    shift_row = modulation[:, layer_width : 2 * layer_width]
    scale_row = modulation[:, 2 * layer_width :]
    base_full, down_full, up_full, head_ref_full, head_pol_full = (
        lax.all_gather(frozen_output_weight, "fsdp", axis=1, tiled=True),
        lax.all_gather(adapter_down_weight, "fsdp", axis=1, tiled=True),
        lax.all_gather(adapter_up_weight, "fsdp", axis=1, tiled=True),
        lax.all_gather(reference_head, "fsdp", axis=1, tiled=True),
        lax.all_gather(policy_head, "fsdp", axis=1, tiled=True),
    )
    rows_ref = reference_attention.reshape(-1, feature_index)
    policy_rows = policy_attention.reshape(-1, feature_index)
    stream_ref = reference_residual.reshape(-1, layer_width)
    stream_pol = policy_residual.reshape(-1, layer_width)
    target = (noise - latent).reshape(-1, channel_count)
    sign_rows = jnp.concatenate(
        [jnp.ones((tok_seq, 1), jnp.float32), -jnp.ones((tok_seq, 1), jnp.float32)], axis=0
    )
    proj_ref = jnp.dot(rows_ref, base_full, preferred_element_type=jnp.float32)
    normed_ref, inv_ref, z_ref, pred_ref = final_layer(
        proj_ref, stream_ref, gate_row, shift_row, scale_row, head_ref_full
    )
    part_ref = member_errors(pred_ref, target, scale_total)
    low_rank_rows = contracted_columns(policy_rows, down_full).astype(jnp.bfloat16)
    policy_projection = jnp.dot(
        policy_rows, base_full, preferred_element_type=jnp.float32
    ) + jnp.dot(low_rank_rows, up_full, preferred_element_type=jnp.float32)
    normed_pol, inv_pol, z_pol, pred_pol = final_layer(
        policy_projection, stream_pol, gate_row, shift_row, scale_row, head_pol_full
    )
    part_pol = member_errors(pred_pol, target, scale_total)
    local_margin = part_pol[0] - part_ref[0] - (part_pol[1] - part_ref[1])
    margin = lax.psum(local_margin, "seq")
    loss = jax.nn.softplus(beta * margin).reshape(1)
    weight_pair = jax.nn.sigmoid(beta * margin)
    dpred = (sign_rows * weight_pair * 2.0 * (pred_pol - target)).astype(jnp.bfloat16)
    head_part = contract_rows(dpred, z_pol)
    dz_rows = jnp.dot(dpred, head_pol_full, preferred_element_type=jnp.float32)
    dn_rows = dz_rows * (1.0 + scale_row)
    dstream = inv_pol * (
        dn_rows
        - jnp.mean(dn_rows, axis=1, keepdims=True)
        - normed_pol * jnp.mean(dn_rows * normed_pol, axis=1, keepdims=True)
    )
    grad_resid = dstream.astype(jnp.bfloat16).reshape(policy_residual.shape)
    projection_gradient = (gate_row * dstream).astype(jnp.bfloat16)
    up_part = contract_rows(low_rank_rows, projection_gradient)
    low_rank_gradient = contracted_columns(projection_gradient, up_full).astype(jnp.bfloat16)
    down_part = contract_rows(low_rank_gradient, policy_rows)
    grad_attn = (
        (
            contracted_columns(projection_gradient, base_full)
            + jnp.dot(low_rank_gradient, down_full, preferred_element_type=jnp.float32)
        )
        .astype(jnp.bfloat16)
        .reshape(policy_attention.shape)
    )
    summed = (
        lax.psum(down_part.astype(jnp.bfloat16), "seq").astype(jnp.float32),
        lax.psum(up_part.astype(jnp.bfloat16), "seq").astype(jnp.float32),
        lax.psum(head_part.astype(jnp.bfloat16), "seq").astype(jnp.float32),
    )
    down_sum, up_sum, head_sum = (
        lax.psum_scatter(
            summed[0].astype(jnp.bfloat16), "fsdp", scatter_dimension=1, tiled=True
        ).astype(jnp.float32),
        lax.psum_scatter(
            summed[1].astype(jnp.bfloat16), "fsdp", scatter_dimension=1, tiled=True
        ).astype(jnp.float32),
        lax.psum_scatter(
            summed[2].astype(jnp.bfloat16), "fsdp", scatter_dimension=1, tiled=True
        ).astype(jnp.float32),
    )
    local_squares = (
        jnp.sum(down_sum * down_sum) + jnp.sum(up_sum * up_sum) + jnp.sum(head_sum * head_sum)
    )
    total = lax.psum(local_squares, "fsdp")
    upper_limit = math.sqrt(
        adapter_down_weight.shape[0] * feature_index
        + adapter_up_weight.shape[0] * layer_width
        + channel_count * layer_width
    )
    factor = jnp.minimum(1.0, upper_limit / jnp.sqrt(total + 1e-12))
    return (loss, factor * down_sum, factor * up_sum, factor * head_sum, grad_resid, grad_attn)


def solution(mesh):
    in_specs = (
        P("fsdp"),
        P("fsdp", None),
        P("fsdp", "seq"),
        P("fsdp", None, "seq", None),
        P("fsdp", None, "seq", None),
        P("fsdp", None, "seq", None),
        P("fsdp", None, "seq", None),
        P("fsdp", None, "seq", None),
        P("fsdp", None, "seq", None),
        P(None, "fsdp"),
        P(None, "fsdp"),
        P(None, "fsdp"),
        P(None, "fsdp"),
        P(None, "fsdp"),
    )
    out_specs = (
        P("fsdp"),
        P(None, "fsdp"),
        P(None, "fsdp"),
        P(None, "fsdp"),
        P("fsdp", None, "seq", None),
        P("fsdp", None, "seq", None),
    )
    return jax.shard_map(local, mesh=mesh, in_specs=in_specs, out_specs=out_specs, check_vma=False)
```

profile of v0, /device:TPU:0, one launch (start us, length us, event | category | flops | bytes accessed | tf_op | source)
XLA Modules:
  0.0 396.3 jit_solution(11403654246023301120)
XLA Ops:
  7.3 0.7 all-gather.2.cloned.1.call-update
  8.7 0.2 fusion.13
  9.0 0.5 broadcast.112
  9.5 0.7 reduce
  10.2 0.6 reshape.126
  10.8 6.3 %all-to-all-start = ((bf16[4,2,384]{2,1,0:T(2,128)(2,1)}), bf16[4,2,384]{2,1,0:T(2,128)(2,1)S(1)}, u32[]{:S(2)}, u32[]{:S(2)}) async-start(bf16[4,2,384]{2,1,0:T(2,128)(2,1)} %reshape.126), calls=%async_computation | async-start | bytes 12288 | tf_op jit(solution)/shard_map/all_to_all | solution.py:72
  17.1 15.6 %all_gather.20 = bf16[64,1536]{1,0:T(8,128)(2,1)S(1)} all-gather(bf16[64,384]{1,0:T(8,128)(2,1)S(1)} %copy-done.25), channel_id=1, replica_groups=mesh['fsdp'=4,'seq'=8] {'fsdp'}, dimensions={1}, use_global_device_ids=true | all-gather | bytes 245760 | tf_op jit(solution)/shard_map/all_gather | solution.py:81
  32.8 29.9 %all_gather.21 = bf16[64,3072]{1,0:T(8,128)(2,1)} all-gather(bf16[64,768]{1,0:T(8,128)(2,1)S(1)} %copy-done.18), channel_id=1, replica_groups=mesh['fsdp'=4,'seq'=8] {'fsdp'}, dimensions={1}, use_global_device_ids=true | all-gather | bytes 491520 | tf_op jit(solution)/shard_map/all_gather | solution.py:82
  62.7 21.7 %all_gather.22 = bf16[64,3072]{1,0:T(8,128)(2,1)} all-gather(bf16[64,768]{1,0:T(8,128)(2,1)S(1)} %copy-done.19), channel_id=1, replica_groups=mesh['fsdp'=4,'seq'=8] {'fsdp'}, dimensions={1}, use_global_device_ids=true | all-gather | bytes 491520 | tf_op jit(solution)/shard_map/all_gather | solution.py:84
  84.4 0.9 convolution_convert_fusion.4
  85.3 28.9 %all_gather.23 = bf16[64,3072]{1,0:T(8,128)(2,1)} all-gather(bf16[64,768]{1,0:T(8,128)(2,1)S(1)} %copy-done.20), channel_id=1, replica_groups=mesh['fsdp'=4,'seq'=8] {'fsdp'}, dimensions={1}, use_global_device_ids=true | all-gather | bytes 491520 | tf_op jit(solution)/shard_map/all_gather | solution.py:83
  114.2 0.7 copy.23
  114.9 0.6 dynamic-slice
  115.5 0.3 fusion.10
  115.9 24.3 %all-reduce = f32[4,1152]{1,0:T(4,128)S(1)} all-reduce(f32[4,1152]{1,0:T(4,128)S(1)} %fusion.10), channel_id=2, replica_groups=mesh['fsdp'=4,'seq'=8] {'fsdp'}, use_global_device_ids=true, to_apply=%region_0.1.clone | all-reduce | flops 4608 | bytes 36864
  140.1 0.7 constant_dynamic-slice_fusion
  140.8 9.2 %all_gather.18 = f32[1,9216]{1,0:T(1,128)S(1)} all-gather(f32[1,1152]{1,0:T(1,128)S(1)} %constant_dynamic-slice_fusion), channel_id=1, replica_groups=mesh['fsdp'=4,'seq'=8] {'seq'}, dimensions={1}, use_global_device_ids=true | all-gather | bytes 41472 | tf_op jit(solution)/shard_map/all_gather | solution.py:75
  149.9 0.6 slice_add_fusion
  150.5 49.8 %all-gather.2.cloned.1.call-done = bf16[1536,3072]{1,0:T(8,128)(2,1)} async-done(((bf16[1536,768]{1,0:T(8,128)(2,1)}), bf16[1536,3072]{1,0:T(8,128)(2,1)}) %all-gather.2.cloned.1.call-update) | async-done | bytes 9437200 | tf_op jit(solution)/shard_map/all_gather | solution.py:80
  200.4 5.2 %fusion.21 = f32[128,3072]{1,0:T(8,128)S(1)} fusion(bf16[128,1536]{1,0:T(8,128)(2,1)S(1)} %bitcast.49, bf16[1536,3072]{1,0:T(8,128)(2,1)} %all-gather.2.cloned.1.call-done), kind=kOutput, calls=%fused_computation.62 | convolution fusion | flops 1207959552 | bytes 11403264 | tf_op jit(solution)/shard_map/dot_general | solution.py:100
  205.6 0.5 fusion.19
  206.2 0.3 multiply_reduce_fusion.2
  206.5 0.3 copy-done.16
  206.9 0.3 add_convert_fusion.1
  207.2 0.9 copy-done.1
  208.1 1.5 multiply_reduce_fusion.3
  209.6 1.3 reshape.115
  210.9 1.3 reduce_sum.120
  212.3 0.7 broadcast_multiply_fusion.1
  212.9 0.6 fusion.18
  213.5 5.5 %fusion.20 = (f32[128]{0:T(128)S(1)}, f32[128,3072]{1,0:T(8,128)S(1)}) fusion(bf16[128,1536]{1,0:T(8,128)(2,1)} %bitcast.52, bf16[1536,3072]{1,0:T(8,128)(2,1)} %all-gather.2.cloned.1.call-done, f32[3072]{0:T(1024)S(1)} %bitcast.59, bf16[128,3072]{1,0:T(8,128)(2,1)} %bitcast.55), kind=kOutput, calls=%fused_computation.61 | convolution fusion | flops 1209532288 | bytes 12202496 | tf_op jit(solution)/shard_map/dot_general | solution.py:94
  219.1 0.3 multiply_reduce_fusion.1
  219.4 0.6 copy-done.9
  220.0 1.0 fusion.5
  221.0 1.3 reshape.117
  222.3 1.3 reduce_sum.124
  223.6 0.7 broadcast_multiply_fusion
  224.3 0.6 fusion.17
  227.5 14.9 %psum.35 = f32[]{:T(128)} all-reduce(f32[]{:T(128)} %bitcast.10), channel_id=1, replica_groups=mesh['fsdp'=4,'seq'=8] {'seq'}, use_global_device_ids=true, to_apply=%region_9.10 | all-reduce | flops 1 | bytes 8 | tf_op jit(solution)/shard_map/psum | solution.py:108
  243.2 0.7 multiply_multiply_fusion
  243.9 1.6 fusion.15
  245.5 1.4 fusion.16
  247.0 0.9 copy-done.7
  247.9 0.4 convolution_convert_fusion.3
  248.3 0.6 copy-done.12
  248.9 0.9 convolution_convert_fusion.2
  249.8 1.8 copy.24
  251.7 1.8 convolution_convert_fusion
  253.7 1.0 convolution_convert_fusion.1
  254.7 0.2 all-reduce.4.cloned.1.call-start
  255.0 6.9 %fusion.22 = f32[128,1536]{1,0:T(8,128)S(1)} fusion(bf16[128,3072]{1,0:T(8,128)(2,1)S(1)} %multiply_convert_fusion, bf16[1536,3072]{1,0:T(8,128)(2,1)} %all-gather.2.cloned.1.call-done), kind=kOutput, calls=%fused_computation.63 | convolution fusion | flops 1207959552 | bytes 11010048 | tf_op jit(solution)/shard_map/dot_general | solution.py:24
  261.9 1.0 fusion.3
  262.9 6.4 %reduce-scatter.10.cloned.1.call-done = bf16[384,64]{1,0:T(8,128)(2,1)} async-done(((bf16[1536,64]{1,0:T(8,128)(2,1)}), bf16[384,64]{1,0:T(8,128)(2,1)}) %reduce-scatter.10.cloned.1.call-update) | async-done | bytes 49168
  269.3 1.0 copy.25
  270.3 22.9 %psum.40 = bf16[64,384]{1,0:T(8,128)(2,1)S(1)} all-reduce(bf16[64,384]{1,0:T(8,128)(2,1)S(1)} %copy.25), channel_id=1, replica_groups=mesh['fsdp'=4,'seq'=8] {'seq'}, use_global_device_ids=true, to_apply=%region_12.13 | all-reduce | flops 24576 | bytes 98304 | tf_op jit(solution)/shard_map/psum | solution.py:134
  293.2 18.6 %reduce-scatter.6.cloned.1.call-done = bf16[64,768]{1,0:T(8,128)(2,1)} async-done(((bf16[64,3072]{1,0:T(8,128)(2,1)}), bf16[64,768]{1,0:T(8,128)(2,1)}) %reduce-scatter.6.cloned.1.call-update) | async-done | bytes 98320 | tf_op jit(solution)/shard_map/reduce_scatter | solution.py:142
  311.8 0.6 fusion.8
  312.5 54.4 %all-reduce.4.cloned.1.call-done = (bf16[64,768]{1,0:T(8,128)(2,1)}, bf16[64,768]{1,0:T(8,128)(2,1)}) async-done(((bf16[64,768]{1,0:T(8,128)(2,1)}, bf16[64,768]{1,0:T(8,128)(2,1)}), (bf16[64,768]{1,0:T(8,128)(2,1)}, bf16[64,768]{1,0:T(8,128)(2,1)})) %all-reduce.4.cloned.1.call-update) | async-done | bytes 196624 | tf_op jit(solution)/shard_map/psum | solution.py:135
  366.9 1.5 fusion.7
  368.4 1.5 fusion.6
  371.9 12.2 %psum.39 = f32[]{:T(128)} all-reduce(f32[]{:T(128)S(6)} %add.105), channel_id=1, replica_groups=mesh['fsdp'=4,'seq'=8] {'fsdp'}, use_global_device_ids=true, to_apply=%region_21.22 | all-reduce | flops 1 | bytes 8 | tf_op jit(solution)/shard_map/psum | solution.py:152
  384.8 0.7 convert_multiply_fusion.4
  385.4 1.6 convert_multiply_fusion
  387.0 1.6 convert_multiply_fusion.2
  (77 shorter events, 0.6 us)
Async XLA Ops:
  7.2 108.3 %copy-start = (bf16[768,1152]{1,0:T(8,128)(2,1)S(1)}, bf16[768,1152]{1,0:T(8,128)(2,1)}, u32[]{:S(2)}) copy-start(bf16[768,1152]{1,0:T(8,128)(2,1)} %param.16) | copy-start | bytes 5308420
  7.2 1.7 copy-start.26
  7.2 9.9 %copy-start.25 = (bf16[64,384]{1,0:T(8,128)(2,1)S(1)}, bf16[64,384]{1,0:T(8,128)(2,1)}, u32[]{:S(2)}) copy-start(bf16[64,384]{1,0:T(8,128)(2,1)} %param.24) | copy-start | bytes 147460
  7.2 25.6 %copy-start.18 = (bf16[64,768]{1,0:T(8,128)(2,1)S(1)}, bf16[64,768]{1,0:T(8,128)(2,1)}, u32[]{:S(2)}) copy-start(bf16[64,768]{1,0:T(8,128)(2,1)} %param.25) | copy-start | bytes 294916
  7.2 55.5 %copy-start.19 = (bf16[64,768]{1,0:T(8,128)(2,1)S(1)}, bf16[64,768]{1,0:T(8,128)(2,1)}, u32[]{:S(2)}) copy-start(bf16[64,768]{1,0:T(8,128)(2,1)} %param.27) | copy-start | bytes 294916
  7.2 77.2 %copy-start.3 = (bf16[1,2,64,1536]{3,2,1,0:T(8,128)(2,1)S(1)}, bf16[1,2,64,1536]{3,2,1,0:T(8,128)(2,1)}, u32[]{:S(2)}) copy-start(bf16[1,2,64,1536]{3,2,1,0:T(8,128)(2,1)} %param.18) | copy-start | bytes 1179652
  7.2 78.0 %copy-start.20 = (bf16[64,768]{1,0:T(8,128)(2,1)S(1)}, bf16[64,768]{1,0:T(8,128)(2,1)}, u32[]{:S(2)}) copy-start(bf16[64,768]{1,0:T(8,128)(2,1)} %param.26) | copy-start | bytes 294916
  7.2 193.2 %all-gather.2.cloned.1.call-start = ((), (), s32[]{:S(2)}) async-start(), calls=%async_computation.4 | async-start | bytes 11796480 | tf_op jit(solution)/shard_map/all_gather | solution.py:80
  8.0 106.2 %copy-start.21 = (f32[1,2,64,64]{3,2,1,0:T(8,128)S(1)}, f32[1,2,64,64]{3,2,1,0:T(8,128)}, u32[]{:S(2)}) copy-start(f32[1,2,64,64]{3,2,1,0:T(8,128)} %param.21) | copy-start | bytes 98308
  8.0 106.2 %copy-start.22 = (f32[1,2,64,64]{3,2,1,0:T(8,128)S(1)}, f32[1,2,64,64]{3,2,1,0:T(8,128)}, u32[]{:S(2)}) copy-start(f32[1,2,64,64]{3,2,1,0:T(8,128)} %param.22) | copy-start | bytes 98308
  8.0 106.9 %copy-start.30 = (u32[32]{0:T(128)S(1)}, u32[32]{0:T(128)}, u32[]{:S(2)}) copy-start(u32[32]{0:T(128)} %constant.54) | copy-start | bytes 388
  10.8 104.7 %all-to-all-start = ((bf16[4,2,384]{2,1,0:T(2,128)(2,1)}), bf16[4,2,384]{2,1,0:T(2,128)(2,1)S(1)}, u32[]{:S(2)}, u32[]{:S(2)}) async-start(bf16[4,2,384]{2,1,0:T(2,128)(2,1)} %reshape.126), calls=%async_computation | async-start | bytes 12288 | tf_op jit(solution)/shard_map/all_to_all | solution.py:72
  17.1 252.2 %reduce-scatter.10.cloned.1.call-start = ((), (), s32[]{:S(2)}) async-start(), calls=%async_computation.7 | async-start | bytes 491520
  200.4 5.2 %copy-start.6 = (bf16[64,3072]{1,0:T(8,128)(2,1)S(1)}, bf16[64,3072]{1,0:T(8,128)(2,1)}, u32[]{:S(2)}) copy-start(bf16[64,3072]{1,0:T(8,128)(2,1)} %all_gather.21) | copy-start | bytes 1179652
  200.4 5.2 %copy-start.8 = (bf16[1,2,64,3072]{3,2,1,0:T(8,128)(2,1)S(1)}, bf16[1,2,64,3072]{3,2,1,0:T(8,128)(2,1)}, u32[]{:S(2)}) copy-start(bf16[1,2,64,3072]{3,2,1,0:T(8,128)(2,1)} %param.20) | copy-start | bytes 2359300
  200.4 5.2 %copy-start.10 = (bf16[128,64]{0,1:T(8,128)(2,1)S(1)}, bf16[128,64]{0,1:T(8,128)(2,1)}, u32[]{:S(2)}) copy-start(bf16[128,64]{0,1:T(8,128)(2,1)} %convolution_convert_fusion.4) | copy-start | bytes 49156
  206.1 0.7 copy-start.16
  206.2 0.7 copy-start.23
  206.5 1.6 copy-start.5
  206.5 1.6 copy-start.14
  206.5 3.1 copy-start.27
  207.2 0.9 copy-start.1
  219.0 1.0 copy-start.9
  219.0 1.0 copy-start.15
  219.0 1.0 copy-start.17
  219.1 1.0 copy-start.24
  243.9 1.6 copy-start.29
  243.9 1.6 copy-start.28
  246.9 1.0 copy-start.7
  246.9 2.0 copy-start.4
  247.9 3.8 copy-start.2
  248.3 0.6 copy-start.12
  248.9 4.7 %copy-start.11 = (bf16[128,64]{0,1:T(8,128)(2,1)S(1)}, bf16[128,64]{0,1:T(8,128)(2,1)}, u32[]{:S(2)}) copy-start(bf16[128,64]{0,1:T(8,128)(2,1)} %convolution_convert_fusion.4) | copy-start | bytes 49156
  251.7 41.6 %reduce-scatter.8.cloned.1.call-start = ((), (), s32[]{:S(2)}) async-start(), calls=%async_computation.6 | async-start | bytes 491520 | tf_op jit(solution)/shard_map/reduce_scatter | solution.py:145
  253.5 58.3 %reduce-scatter.6.cloned.1.call-start = ((), (), s32[]{:S(2)}) async-start(), calls=%async_computation.5 | async-start | bytes 491520 | tf_op jit(solution)/shard_map/reduce_scatter | solution.py:142
  254.7 7.2 %copy-start.13 = (bf16[128,64]{0,1:T(8,128)(2,1)S(1)}, bf16[128,64]{0,1:T(8,128)(2,1)}, u32[]{:S(2)}) copy-start(bf16[128,64]{0,1:T(8,128)(2,1)} %copy-done.12) | copy-start | bytes 49156
  254.7 112.1 %all-reduce.4.cloned.1.call-start = ((), (), s32[]{:S(2)}) async-start(), calls=%async_computation.8 | async-start | bytes 393216 | tf_op jit(solution)/shard_map/psum | solution.py:135
Sparse Core Ops, SparseCore 0:
  9.6 190.7 all-gather.1
  251.8 17.4 reduce-scatter.9
  271.6 18.9 reduce-scatter.7
  292.8 19.0 reduce-scatter.5
  314.8 52.0 all-reduce.3
where the time goes:
time: 397 us; the launch traced here: 396 us
  blocking collectives  180 us (45%)
  waiting for transfers between devices  130 us (33%)
  matrix products  28.5 us (7%)
  between operations  22.1 us (6%)
  other arithmetic  16.2 us (4%)
  local copies, waits for them, and re-layouts  13.1 us (3%)
  starting transfers between devices  6.69 us (2%)
    psum x1, waiting for transfers between devices, local(): lax.psum(up_part.astype(jnp.bfloat16), 'seq').astype(jnp.float32)  54.4 us
    all_gather x1, waiting for transfers between devices, local(): lax.all_gather(frozen_output_weight, 'fsdp', axis=1, tiled=True)  49.8 us
    all_gather x1, blocking collectives, local(): lax.all_gather(adapter_up_weight, 'fsdp', axis=1, tiled=True)  29.9 us
    all_gather x1, blocking collectives, local(): lax.all_gather(reference_head, 'fsdp', axis=1, tiled=True)  28.9 us
    unnamed x1, blocking collectives  24.3 us
    psum x1, blocking collectives, local(): lax.psum(down_part.astype(jnp.bfloat16), 'seq').astype(jnp.float32)  22.9 us
    all_gather x1, blocking collectives, local(): lax.all_gather(policy_head, 'fsdp', axis=1, tiled=True)  21.7 us
    reduce_scatter x1, waiting for transfers between devices, local(): lax.psum_scatter(summed[1].astype(jnp.bfloat16), 'fsdp', scatter_dimensio...  18.6 us
  transfers between devices with their start and end apart: 6, of which 4 were waited for; matrix products, arithmetic and copies ran while one was open for 5% of the time, Pallas kernels for 0%

commit v1 on v0

--- a/solution.py
+++ b/solution.py
@@ -132,7 +132,7 @@
     )
     summed = (
         lax.psum(down_part.astype(jnp.bfloat16), "seq").astype(jnp.float32),
-        lax.psum(up_part.astype(jnp.bfloat16), "seq").astype(jnp.float32),
+        jnp.sum(lax.all_gather(up_part.astype(jnp.bfloat16), "seq"), axis=0).astype(jnp.float32),
         lax.psum(head_part.astype(jnp.bfloat16), "seq").astype(jnp.float32),
     )
     down_sum, up_sum, head_sum = (

time: 397 us -> 426 us (1.073)
  waiting for transfers between devices: 130 us -> 156 us
  other arithmetic: 16.2 us -> 22.3 us
    all_gather x0 -> x1, waiting for transfers between devices: none -> 32.7 us  [local(): lax.all_gather(up_part.astype(jnp.bfloat16), 'seq')]
    psum x1, waiting for transfers between devices: 54.4 us -> 28.8 us  [local(): lax.psum(head_part.astype(jnp.bfloat16), 'seq').astype(jnp.float32)]
    reduce_scatter x1, waiting for transfers between devices: 0.02 us -> 9.9 us  [local(): lax.psum_scatter(summed[2].astype(jnp.bfloat16), 'fsdp', scatter_dimensio...]
    unnamed x6 -> x7, waiting for transfers between devices: 7.14 us -> 12.4 us
    unnamed x69 -> x61, local copies, waits for them, and re-layouts: 8.64 us -> 7.37 us
  transfers between devices with their start and end apart: 6 -> 7, of which waited for: 4 -> 6; matrix products, arithmetic and copies ran while one was open for 5% -> 6% of each run, Pallas kernels for 0% -> 0%
where the time goes in v1:
time: 426 us
  blocking collectives  176 us (41%)
  waiting for transfers between devices  156 us (37%)
  matrix products  30 us (7%)
  between operations  22.4 us (5%)
  other arithmetic  22.3 us (5%)
  local copies, waits for them, and re-layouts  11.9 us (3%)
  starting transfers between devices  6.73 us (2%)
    all_gather x1, waiting for transfers between devices, local(): lax.all_gather(frozen_output_weight, 'fsdp', axis=1, tiled=True)  49.8 us
    all_gather x1, waiting for transfers between devices, local(): lax.all_gather(up_part.astype(jnp.bfloat16), 'seq')  32.7 us
    all_gather x1, blocking collectives, local(): lax.all_gather(adapter_up_weight, 'fsdp', axis=1, tiled=True)  29.9 us
    all_gather x1, blocking collectives, local(): lax.all_gather(reference_head, 'fsdp', axis=1, tiled=True)  28.9 us
    psum x1, waiting for transfers between devices, local(): lax.psum(head_part.astype(jnp.bfloat16), 'seq').astype(jnp.float32)  28.8 us
    unnamed x1, blocking collectives  24.3 us
    psum x1, blocking collectives, local(): lax.psum(down_part.astype(jnp.bfloat16), 'seq').astype(jnp.float32)  22.8 us
    reduce_scatter x1, waiting for transfers between devices, local(): lax.psum_scatter(summed[1].astype(jnp.bfloat16), 'fsdp', scatter_dimensio...  22.2 us
  transfers between devices with their start and end apart: 7, of which 6 were waited for; matrix products, arithmetic and copies ran while one was open for 6% of the time, Pallas kernels for 0%

profile of v1, /device:TPU:0, one launch (start us, length us, event | category | flops | bytes accessed | tf_op | source)
XLA Modules:
  0.0 425.5 jit_solution(12629482595744222906)
XLA Ops:
  7.3 0.7 all-gather.4.cloned.1.call-update
  9.0 0.5 broadcast.112
  9.5 0.7 reduce.1
  10.2 0.6 reshape.127
  10.8 6.3 %all-to-all-start = ((bf16[4,2,384]{2,1,0:T(2,128)(2,1)}), bf16[4,2,384]{2,1,0:T(2,128)(2,1)S(1)}, u32[]{:S(2)}, u32[]{:S(2)}) async-start(bf16[4,2,384]{2,1,0:T(2,128)(2,1)} %reshape.127), calls=%async_computation | async-start | bytes 12288 | tf_op jit(solution)/shard_map/all_to_all | solution.py:72
  17.1 15.6 %all_gather.26 = bf16[64,1536]{1,0:T(8,128)(2,1)S(1)} all-gather(bf16[64,384]{1,0:T(8,128)(2,1)S(1)} %copy-done.22), channel_id=1, replica_groups=mesh['fsdp'=4,'seq'=8] {'fsdp'}, dimensions={1}, use_global_device_ids=true | all-gather | bytes 245760 | tf_op jit(solution)/shard_map/all_gather | solution.py:81
  32.8 29.9 %all_gather.27 = bf16[64,3072]{1,0:T(8,128)(2,1)} all-gather(bf16[64,768]{1,0:T(8,128)(2,1)S(1)} %copy-done.15), channel_id=1, replica_groups=mesh['fsdp'=4,'seq'=8] {'fsdp'}, dimensions={1}, use_global_device_ids=true | all-gather | bytes 491520 | tf_op jit(solution)/shard_map/all_gather | solution.py:82
  62.7 21.7 %all_gather.28 = bf16[64,3072]{1,0:T(8,128)(2,1)} all-gather(bf16[64,768]{1,0:T(8,128)(2,1)S(1)} %copy-done.16), channel_id=1, replica_groups=mesh['fsdp'=4,'seq'=8] {'fsdp'}, dimensions={1}, use_global_device_ids=true | all-gather | bytes 491520 | tf_op jit(solution)/shard_map/all_gather | solution.py:84
  84.4 0.9 convolution_convert_fusion.4
  85.3 28.9 %all_gather.29 = bf16[64,3072]{1,0:T(8,128)(2,1)} all-gather(bf16[64,768]{1,0:T(8,128)(2,1)S(1)} %copy-done.17), channel_id=1, replica_groups=mesh['fsdp'=4,'seq'=8] {'fsdp'}, dimensions={1}, use_global_device_ids=true | all-gather | bytes 491520 | tf_op jit(solution)/shard_map/all_gather | solution.py:83
  114.2 0.7 copy.23
  114.9 0.6 dynamic-slice
  115.5 0.3 fusion.10
  115.9 24.3 %all-reduce = f32[4,1152]{1,0:T(4,128)S(1)} all-reduce(f32[4,1152]{1,0:T(4,128)S(1)} %fusion.10), channel_id=3, replica_groups=mesh['fsdp'=4,'seq'=8] {'fsdp'}, use_global_device_ids=true, to_apply=%region_0.1.clone | all-reduce | flops 4608 | bytes 36864
  140.1 0.7 constant_dynamic-slice_fusion
  140.8 9.2 %all_gather.24 = f32[1,9216]{1,0:T(1,128)S(1)} all-gather(f32[1,1152]{1,0:T(1,128)S(1)} %constant_dynamic-slice_fusion), channel_id=1, replica_groups=mesh['fsdp'=4,'seq'=8] {'seq'}, dimensions={1}, use_global_device_ids=true | all-gather | bytes 41472 | tf_op jit(solution)/shard_map/all_gather | solution.py:75
  149.9 0.6 slice_add_fusion
  150.5 49.8 %all-gather.4.cloned.1.call-done = bf16[1536,3072]{1,0:T(8,128)(2,1)} async-done(((bf16[1536,768]{1,0:T(8,128)(2,1)}), bf16[1536,3072]{1,0:T(8,128)(2,1)}) %all-gather.4.cloned.1.call-update) | async-done | bytes 9437200 | tf_op jit(solution)/shard_map/all_gather | solution.py:80
  200.4 5.2 %fusion.21 = f32[128,3072]{1,0:T(8,128)S(1)} fusion(bf16[128,1536]{1,0:T(8,128)(2,1)S(1)} %bitcast.50, bf16[1536,3072]{1,0:T(8,128)(2,1)} %all-gather.4.cloned.1.call-done), kind=kOutput, calls=%fused_computation.62 | convolution fusion | flops 1207959552 | bytes 11403264 | tf_op jit(solution)/shard_map/dot_general | solution.py:100
  205.6 0.5 fusion.19
  206.5 0.3 copy-done.13
  206.9 0.3 add_convert_fusion.1
  207.2 0.9 copy-done.1
  208.1 1.5 multiply_reduce_fusion.3
  209.6 1.3 reshape.115
  210.9 1.3 reduce_sum.132
  212.2 0.7 broadcast_multiply_fusion.1
  212.9 0.6 fusion.18
  213.5 5.5 %fusion.20 = (f32[128]{0:T(128)S(1)}, f32[128,3072]{1,0:T(8,128)S(1)}) fusion(bf16[128,1536]{1,0:T(8,128)(2,1)} %bitcast.54, bf16[1536,3072]{1,0:T(8,128)(2,1)} %all-gather.4.cloned.1.call-done, f32[3072]{0:T(1024)S(1)} %bitcast.61, bf16[128,3072]{1,0:T(8,128)(2,1)} %bitcast.57), kind=kOutput, calls=%fused_computation.61 | convolution fusion | flops 1209532288 | bytes 12202496 | tf_op jit(solution)/shard_map/dot_general | solution.py:94
  219.4 0.6 copy-done.8
  220.0 1.1 fusion.5
  221.1 1.3 reshape.117
  222.4 1.4 reduce_sum.136
  223.8 0.7 broadcast_multiply_fusion
  224.5 0.6 fusion.17
  227.7 14.9 %psum.28 = f32[]{:T(128)} all-reduce(f32[]{:T(128)} %bitcast.10), channel_id=1, replica_groups=mesh['fsdp'=4,'seq'=8] {'seq'}, use_global_device_ids=true, to_apply=%region_9.10 | all-reduce | flops 1 | bytes 8 | tf_op jit(solution)/shard_map/psum | solution.py:108
  243.4 0.7 multiply_multiply_fusion
  244.0 0.5 copy-done.25
  244.5 2.2 convolution_convert_fusion
  246.7 3.2 fusion.15
  250.0 0.7 broadcast_multiply_fusion.3
  250.7 0.7 broadcast_multiply_fusion.2
  251.3 2.8 fusion.16
  254.3 0.6 copy-done.10
  254.9 1.0 convolution_convert_fusion.1
  256.0 0.4 convolution_convert_fusion.3
  256.6 1.0 copy.24
  257.6 9.9 %reduce-scatter.8.cloned.1.call-done = bf16[64,768]{1,0:T(8,128)(2,1)} async-done(((bf16[64,3072]{1,0:T(8,128)(2,1)}), bf16[64,768]{1,0:T(8,128)(2,1)}) %reduce-scatter.8.cloned.1.call-update) | async-done | bytes 98320 | tf_op jit(solution)/shard_map/reduce_scatter | solution.py:145
  267.8 32.7 %all-gather.6.cloned.1.call-done = bf16[512,3072]{1,0:T(8,128)(2,1)} async-done(((bf16[64,3072]{1,0:T(8,128)(2,1)}), bf16[512,3072]{1,0:T(8,128)(2,1)}) %all-gather.6.cloned.1.call-update) | async-done | bytes 3145744 | tf_op jit(solution)/shard_map/all_gather | solution.py:135
  300.5 3.3 reduce_sum.140
  303.8 6.9 %fusion.22 = f32[128,1536]{1,0:T(8,128)S(1)} fusion(bf16[128,3072]{1,0:T(8,128)(2,1)S(1)} %multiply_convert_fusion, bf16[1536,3072]{1,0:T(8,128)(2,1)} %all-gather.4.cloned.1.call-done), kind=kOutput, calls=%fused_computation.63 | convolution fusion | flops 1207959552 | bytes 11010048 | tf_op jit(solution)/shard_map/dot_general | solution.py:24
  310.8 1.0 fusion.3
  311.9 11.6 %reduce-scatter.10.cloned.1.call-done = bf16[384,64]{1,0:T(8,128)(2,1)} async-done(((bf16[1536,64]{1,0:T(8,128)(2,1)}), bf16[384,64]{1,0:T(8,128)(2,1)}) %reduce-scatter.10.cloned.1.call-update) | async-done | bytes 49168
  323.5 1.0 copy.25
  324.5 22.8 %psum.32 = bf16[64,384]{1,0:T(8,128)(2,1)S(1)} all-reduce(bf16[64,384]{1,0:T(8,128)(2,1)S(1)} %copy.25), channel_id=1, replica_groups=mesh['fsdp'=4,'seq'=8] {'seq'}, use_global_device_ids=true, to_apply=%region_12.13 | all-reduce | flops 24576 | bytes 98304 | tf_op jit(solution)/shard_map/psum | solution.py:134
  347.2 0.6 fusion.8
  347.9 28.8 %all-reduce.3.cloned.1.call-done = bf16[64,768]{1,0:T(8,128)(2,1)} async-done(((bf16[64,768]{1,0:T(8,128)(2,1)}), bf16[64,768]{1,0:T(8,128)(2,1)}) %all-reduce.3.cloned.1.call-update) | async-done | bytes 98320 | tf_op jit(solution)/shard_map/psum | solution.py:136
  376.7 1.5 fusion.7
  378.2 22.2 %reduce-scatter.6.cloned.1.call-done = bf16[64,768]{1,0:T(8,128)(2,1)} async-done(((bf16[64,3072]{1,0:T(8,128)(2,1)}), bf16[64,768]{1,0:T(8,128)(2,1)}) %reduce-scatter.6.cloned.1.call-update) | async-done | bytes 98320 | tf_op jit(solution)/shard_map/reduce_scatter | solution.py:142
  400.4 1.5 fusion.6
  403.9 9.1 %psum.31 = f32[]{:T(128)} all-reduce(f32[]{:T(128)S(6)} %add.103), channel_id=1, replica_groups=mesh['fsdp'=4,'seq'=8] {'fsdp'}, use_global_device_ids=true, to_apply=%region_21.22 | all-reduce | flops 1 | bytes 8 | tf_op jit(solution)/shard_map/psum | solution.py:152
  413.7 0.7 convert_multiply_fusion.4
  414.4 1.6 convert_multiply_fusion
  415.9 1.6 convert_multiply_fusion.2
  (73 shorter events, 1.8 us)
Async XLA Ops:
  7.2 108.3 %copy-start = (bf16[768,1152]{1,0:T(8,128)(2,1)S(1)}, bf16[768,1152]{1,0:T(8,128)(2,1)}, u32[]{:S(2)}) copy-start(bf16[768,1152]{1,0:T(8,128)(2,1)} %param.16) | copy-start | bytes 5308420
  7.2 1.7 copy-start.23
  7.2 9.9 %copy-start.22 = (bf16[64,384]{1,0:T(8,128)(2,1)S(1)}, bf16[64,384]{1,0:T(8,128)(2,1)}, u32[]{:S(2)}) copy-start(bf16[64,384]{1,0:T(8,128)(2,1)} %param.24) | copy-start | bytes 147460
  7.2 25.6 %copy-start.15 = (bf16[64,768]{1,0:T(8,128)(2,1)S(1)}, bf16[64,768]{1,0:T(8,128)(2,1)}, u32[]{:S(2)}) copy-start(bf16[64,768]{1,0:T(8,128)(2,1)} %param.25) | copy-start | bytes 294916
  7.2 55.5 %copy-start.16 = (bf16[64,768]{1,0:T(8,128)(2,1)S(1)}, bf16[64,768]{1,0:T(8,128)(2,1)}, u32[]{:S(2)}) copy-start(bf16[64,768]{1,0:T(8,128)(2,1)} %param.27) | copy-start | bytes 294916
  7.2 77.2 %copy-start.2 = (bf16[1,2,64,1536]{3,2,1,0:T(8,128)(2,1)S(1)}, bf16[1,2,64,1536]{3,2,1,0:T(8,128)(2,1)}, u32[]{:S(2)}) copy-start(bf16[1,2,64,1536]{3,2,1,0:T(8,128)(2,1)} %param.18) | copy-start | bytes 1179652
  7.2 78.0 %copy-start.17 = (bf16[64,768]{1,0:T(8,128)(2,1)S(1)}, bf16[64,768]{1,0:T(8,128)(2,1)}, u32[]{:S(2)}) copy-start(bf16[64,768]{1,0:T(8,128)(2,1)} %param.26) | copy-start | bytes 294916
  7.2 193.2 %all-gather.4.cloned.1.call-start = ((), (), s32[]{:S(2)}) async-start(), calls=%async_computation.4 | async-start | bytes 11796480 | tf_op jit(solution)/shard_map/all_gather | solution.py:80
  8.0 106.2 %copy-start.18 = (f32[1,2,64,64]{3,2,1,0:T(8,128)S(1)}, f32[1,2,64,64]{3,2,1,0:T(8,128)}, u32[]{:S(2)}) copy-start(f32[1,2,64,64]{3,2,1,0:T(8,128)} %param.21) | copy-start | bytes 98308
  8.0 106.2 %copy-start.19 = (f32[1,2,64,64]{3,2,1,0:T(8,128)S(1)}, f32[1,2,64,64]{3,2,1,0:T(8,128)}, u32[]{:S(2)}) copy-start(f32[1,2,64,64]{3,2,1,0:T(8,128)} %param.22) | copy-start | bytes 98308
  8.0 106.9 %copy-start.26 = (u32[32]{0:T(128)S(1)}, u32[32]{0:T(128)}, u32[]{:S(2)}) copy-start(u32[32]{0:T(128)} %constant.56) | copy-start | bytes 388
  10.8 104.7 %all-to-all-start = ((bf16[4,2,384]{2,1,0:T(2,128)(2,1)}), bf16[4,2,384]{2,1,0:T(2,128)(2,1)S(1)}, u32[]{:S(2)}, u32[]{:S(2)}) async-start(bf16[4,2,384]{2,1,0:T(2,128)(2,1)} %reshape.127), calls=%async_computation | async-start | bytes 12288 | tf_op jit(solution)/shard_map/all_to_all | solution.py:72
  17.1 250.4 %reduce-scatter.8.cloned.1.call-start = ((), (), s32[]{:S(2)}) async-start(), calls=%async_computation.7 | async-start | bytes 491520 | tf_op jit(solution)/shard_map/reduce_scatter | solution.py:145
  200.4 5.2 %copy-start.5 = (bf16[64,3072]{1,0:T(8,128)(2,1)S(1)}, bf16[64,3072]{1,0:T(8,128)(2,1)}, u32[]{:S(2)}) copy-start(bf16[64,3072]{1,0:T(8,128)(2,1)} %all_gather.27) | copy-start | bytes 1179652
  200.4 5.2 %copy-start.7 = (bf16[1,2,64,3072]{3,2,1,0:T(8,128)(2,1)S(1)}, bf16[1,2,64,3072]{3,2,1,0:T(8,128)(2,1)}, u32[]{:S(2)}) copy-start(bf16[1,2,64,3072]{3,2,1,0:T(8,128)(2,1)} %param.20) | copy-start | bytes 2359300
  200.4 5.2 %copy-start.9 = (bf16[128,64]{0,1:T(8,128)(2,1)S(1)}, bf16[128,64]{0,1:T(8,128)(2,1)}, u32[]{:S(2)}) copy-start(bf16[128,64]{0,1:T(8,128)(2,1)} %convolution_convert_fusion.4) | copy-start | bytes 49156
  206.1 0.7 copy-start.13
  206.2 0.7 copy-start.20
  206.5 1.6 copy-start.4
  206.5 1.6 copy-start.11
  206.5 3.1 copy-start.24
  207.2 0.9 copy-start.1
  219.0 1.0 copy-start.8
  219.0 1.0 copy-start.12
  219.0 1.0 copy-start.14
  219.0 1.0 copy-start.21
  244.0 0.5 copy-start.25
  250.0 50.5 %all-gather.6.cloned.1.call-start = ((), (), s32[]{:S(2)}) async-start(), calls=%async_computation.6 | async-start | bytes 3538944 | tf_op jit(solution)/shard_map/all_gather | solution.py:135
  254.2 0.7 copy-start.10
  254.2 1.8 copy-start.6
  254.9 1.5 copy-start.3
  255.9 67.6 %reduce-scatter.10.cloned.1.call-start = ((), (), s32[]{:S(2)}) async-start(), calls=%async_computation.9 | async-start | bytes 491520
  257.6 119.1 %all-reduce.3.cloned.1.call-start = ((), (), s32[]{:S(2)}) async-start(), calls=%async_computation.8 | async-start | bytes 196608 | tf_op jit(solution)/shard_map/psum | solution.py:136
  267.5 132.9 %reduce-scatter.6.cloned.1.call-start = ((), (), s32[]{:S(2)}) async-start(), calls=%async_computation.5 | async-start | bytes 491520 | tf_op jit(solution)/shard_map/reduce_scatter | solution.py:142
Sparse Core Ops, SparseCore 0:
  9.6 190.7 all-gather.3
  250.1 17.3 reduce-scatter.7
  270.0 30.4 all-gather.5
  302.6 20.8 reduce-scatter.9
  326.4 50.2 all-reduce.2
  378.8 21.5 reduce-scatter.5
